TPU v7x, 256 devices: a whole 4x4x8 slice. The times are simulated.
256 devices in a mesh: dp: 128 (over y, x_lo, z, core), rep: 2 (over x_hi).
Axes of the slice: x: 4 (x_hi: 2, x_lo: 2; x = x_hi * 2 + x_lo), y: 4, z: 8, core: 2. Of those that a mesh axis runs over, the one named last changes fastest.
Arguments:
- gate_pre: bfloat16 [2, 16384, 5632], P(None, 'dp', 'rep'), may hold values from -8 to 8
- up_pre: bfloat16 [2, 16384, 5632], P(None, 'dp', 'rep'), may hold values from -6 to 6
- out_grad: bfloat16 [2, 16384, 1024], P(None, 'dp'), may hold values from -24 to 24
- master: float32 [1024, 5632], P('dp', 'rep'), may hold values from -0.078125 to 0.078125
- moment_one: float32 [1024, 5632], P('dp', 'rep'), may hold values from -0.02 to 0.02
- moment_two: float32 [1024, 5632], P('dp', 'rep'), may hold values from 1e-06 to 1e-05
Outputs:
- layer_out: bfloat16 [2, 16384, 1024], P(None, 'dp', 'rep')
- gate_grad: bfloat16 [2, 16384, 5632], P(None, 'dp', 'rep')
- up_grad: bfloat16 [2, 16384, 5632], P(None, 'dp', 'rep')
- master_new: float32 [1024, 5632], P('dp', 'rep')
- moment_one_new: float32 [1024, 5632], P('dp', 'rep')
- moment_two_new: float32 [1024, 5632], P('dp', 'rep')
All inputs are finite; a program needn't handle non-finite values.
Results may differ from a plain program's by a relative error of at most 0.0048.
The roundings to bfloat16 on the way count: a program that leaves them out, or rounds other values in their place, can miss the bound.
Values may be sent and summed in bfloat16 or wider, within the bound.
A program may use at most 128 MiB of HBM per device.

v0:
```python
import jax
import jax.numpy as jnp
from jax import lax
from jax.sharding import Mesh
from jax.sharding import PartitionSpec as P

DP = ("dp_0", "dp_1", "dp_2", "dp_3")
first_power = 2.6561398887587544e-05
second_power = 0.005920529220333997


def in_blocks(x, dim, peers):
    before, after = (x.shape[:dim], x.shape[dim + 1 :])
    return jnp.moveaxis(x.reshape(*before, peers, -1, *after), dim, 0)


def sent_and_summed(x, axis, dim):
    peers = lax.axis_size(axis)
    parts = lax.all_to_all(in_blocks(x, dim, peers), axis, 0, 0, tiled=True)
    return jnp.sum(parts, axis=0)


def sum_by_chip_2(x, chips, core, dim):
    sizes = (lax.axis_size(chips), lax.axis_size(core))
    parts = in_blocks(x, dim, sizes[0] * sizes[1])
    inside = parts.shape[1:]
    parts = parts.reshape(*sizes, *inside).swapaxes(0, 1).reshape(-1, *inside)
    parts = lax.psum_scatter(parts, core, scatter_dimension=0, tiled=True)
    return lax.psum_scatter(parts, chips, scatter_dimension=0, tiled=True)[0]


def grad_rows(cotangent, hidden):
    return lax.dot_general(
        cotangent, hidden, (((0,), (0,)), ((), ())), preferred_element_type=jnp.float32
    )


def on_device(gate_pre, up_pre, out_grad, master, moment_one, moment_two):
    shard_bf = master.astype(jnp.bfloat16)
    weights = lax.all_gather(shard_bf, DP, axis=0, tiled=True)
    micro = gate_pre.shape[0]
    total = micro * gate_pre.shape[1] * lax.axis_size(DP)
    own_rows = master.shape[0]
    outs_list = []
    gate_list = []
    up_list = []
    hidden_list = []
    grad_sum = None
    for index in range(micro):
        gate = gate_pre[index].astype(jnp.float32)
        up_val = up_pre[index].astype(jnp.float32)
        sig = jax.nn.sigmoid(gate)
        hidden = (gate * sig * up_val).astype(jnp.bfloat16)
        hidden_list.append(hidden)
        partial_out = lax.dot_general(
            hidden, weights, (((1,), (1,)), ((), ())), preferred_element_type=jnp.float32
        )
        outs_list.append(sent_and_summed(partial_out, "rep", 1).astype(jnp.bfloat16))
        hid_grad = jnp.dot(out_grad[index], weights, preferred_element_type=jnp.float32)
        gate_list.append(
            (hid_grad * up_val * sig * (1.0 + gate * (1.0 - sig))).astype(jnp.bfloat16)
        )
        up_list.append((hid_grad * gate * sig).astype(jnp.bfloat16))

        def single_term(start, count, cotangent=out_grad[index], current=hidden):
            return grad_rows(cotangent, current)

        shard_grad = sum_by_chip_2(
            single_term(
                jnp.int32(0),
                own_rows * lax.axis_size(("dp_0", "dp_1", "dp_2")) * lax.axis_size("dp_3"),
            ),
            ("dp_0", "dp_1", "dp_2"),
            "dp_3",
            0,
        )
        grad_sum = shard_grad if grad_sum is None else grad_sum + shard_grad
    main_grad = grad_sum / jnp.float32(total)
    first = 0.9 * moment_one + 0.1 * main_grad
    second = 0.95 * moment_two + 0.05 * main_grad * main_grad
    update = first / (1.0 - first_power) / (jnp.sqrt(second / (1.0 - second_power)) + 1e-08)
    master_new = master - 0.003 * (update + 0.1 * master)
    return (
        jnp.stack(outs_list),
        jnp.stack(gate_list),
        jnp.stack(up_list),
        master_new,
        first,
        second,
    )


def solution(mesh):
    torus = Mesh(
        mesh.devices.reshape(4, 2, 8, 2, mesh.shape["rep"]), ("dp_0", "dp_1", "dp_2", "dp_3", "rep")
    )
    return jax.shard_map(
        on_device,
        mesh=torus,
        in_specs=(
            P(None, DP, "rep"),
            P(None, DP, "rep"),
            P(None, DP, None),
            P(DP, "rep"),
            P(DP, "rep"),
            P(DP, "rep"),
        ),
        out_specs=(
            P(None, DP, "rep"),
            P(None, DP, "rep"),
            P(None, DP, "rep"),
            P(DP, "rep"),
            P(DP, "rep"),
            P(DP, "rep"),
        ),
        check_vma=False,
    )
```

profile of v0, /device:TPU:32, one launch (start us, length us, event | category | flops | bytes accessed | tf_op | source)
XLA Modules:
  0.0 641.3 jit_solution(1135383162872716029)
XLA Ops:
  7.2 0.0 copy-start
  7.2 0.0 copy-start.1
  7.2 0.0 copy-start.3
  7.2 0.0 reduce-scatter.5.cloned.1.call-start
  7.2 3.2 fusion.37
  10.5 0.0 copy-done
  10.5 0.0 copy-done.1
  10.5 6.0 convolution_add_fusion
  16.5 9.5 %copy.12 = f32[2,64,8,2816]{3,2,1,0:T(8,128)} copy(f32[2,64,8,2816]{3,2,0,1:T(8,128)} %bitcast.143) | data formatting | bytes 23068672 | tf_op jit(solution)/shard_map/add | solution.py:77
  26.0 0.0 reduce-scatter.5.cloned.1.call-update
  26.0 0.0 reduce-scatter.3.cloned.1.call-start
  26.1 27.0 %reduce-scatter.5.cloned.1.call-done = f32[64,8,2816]{2,1,0:T(8,128)} async-done(((f32[128,8,2816]{2,1,0:T(8,128)}), f32[64,8,2816]{2,1,0:T(8,128)}) %reduce-scatter.5.cloned.1.call-update) | async-done | bytes 5767184 | tf_op jit(solution)/shard_map/reduce_scatter | solution.py:28
  53.1 0.0 reduce-scatter.3.cloned.1.call-update
  53.1 0.0 all-gather.2.cloned.1.call-start
  53.1 329.1 %reduce-scatter.3.cloned.1.call-done = f32[1,8,2816]{2,1,0:T(8,128)} async-done(((f32[64,8,2816]{2,1,0:T(8,128)}), f32[1,8,2816]{2,1,0:T(8,128)}) %reduce-scatter.3.cloned.1.call-update) | async-done | bytes 90128 | tf_op jit(solution)/shard_map/reduce_scatter | solution.py:29
  382.3 1.6 multiply_subtract_fusion
  383.9 0.0 all-gather.2.cloned.1.call-update
  384.0 216.6 %all-gather.2.cloned.1.call-done = bf16[1024,2816]{1,0:T(8,128)(2,1)} async-done(((bf16[8,2816]{1,0:T(8,128)(2,1)}), bf16[1024,2816]{1,0:T(8,128)(2,1)}) %all-gather.2.cloned.1.call-update) | async-done | bytes 5767184 | tf_op jit(solution)/shard_map/all_gather | solution.py:40
  600.5 5.4 convolution_bitcast_fusion
  605.9 4.3 all-to-all-start.1
  610.2 3.8 fusion.44
  614.0 0.1 slice-done.1
  614.2 0.4 copy-done.2
  614.6 0.1 copy-done.4
  614.7 3.1 fusion.40
  617.8 2.8 convolution_bitcast_fusion.1
  620.6 0.0 all-to-all-done.1
  620.6 4.9 all-to-all-start
  625.5 0.0 copy-done.5
  625.5 3.4 pad_maximum_fusion
  628.9 5.0 all-to-all-done
  634.0 0.7 pad_maximum_fusion.2
  (16 shorter events, 0.1 us)
Async XLA Ops:
  7.2 3.3 copy-start
  7.2 3.3 copy-start.1
  7.2 3.3 copy-start.3
  7.2 45.9 %reduce-scatter.5.cloned.1.call-start = ((), (), s32[]{:S(2)}) async-start(), calls=%async_computation.6 | async-start | bytes 17301504 | tf_op jit(solution)/shard_map/reduce_scatter | solution.py:28
  26.0 356.2 %reduce-scatter.3.cloned.1.call-start = ((), (), s32[]{:S(2)}) async-start(), calls=%async_computation.5 | async-start | bytes 5857280 | tf_op jit(solution)/shard_map/reduce_scatter | solution.py:29
  53.1 329.2 %copy-start.6 = (f32[8,2816]{1,0:T(8,128)S(1)}, f32[8,2816]{1,0:T(8,128)}, u32[]{:S(2)}) copy-start(f32[8,2816]{1,0:T(8,128)} %param.9) | copy-start | bytes 270340
  53.1 329.2 %copy-start.7 = (f32[8,2816]{1,0:T(8,128)S(1)}, f32[8,2816]{1,0:T(8,128)}, u32[]{:S(2)}) copy-start(f32[8,2816]{1,0:T(8,128)} %param.10) | copy-start | bytes 270340
  53.1 329.2 %copy-start.8 = (f32[8,2816]{1,0:T(8,128)S(1)}, f32[8,2816]{1,0:T(8,128)}, u32[]{:S(2)}) copy-start(f32[8,2816]{1,0:T(8,128)} %param.11) | copy-start | bytes 270340
  53.1 547.4 %all-gather.2.cloned.1.call-start = ((), (), s32[]{:S(2)}) async-start(), calls=%async_computation.4 | async-start | bytes 5812224 | tf_op jit(solution)/shard_map/all_gather | solution.py:40
  605.9 8.1 %slice-start = ((s8[5767168]{0:T(1024)(128)(4,1)}), s8[1572864]{0:T(1024)(128)(4,1)S(1)}, s32[]{:S(2)}) async-start(s8[5767168]{0:T(1024)(128)(4,1)} %bitcast.146), calls=%async_computation.7 | async-start | bytes 3145728
  605.9 14.6 %all-to-all-start.1 = ((f32[2,128,512]{2,1,0:T(8,128)}), f32[2,128,512]{2,1,0:T(8,128)S(1)}, u32[]{:S(2)}, u32[]{:S(2)}) async-start(f32[2,128,512]{2,1,0:T(8,128)} %convolution_bitcast_fusion), calls=%async_computation.1 | async-start | bytes 1048576 | tf_op jit(solution)/shard_map/all_to_all | solution.py:19
  610.2 3.9 slice-start.1
  610.2 4.4 copy-start.2
  610.2 4.5 copy-start.4
  620.6 4.9 copy-start.5
  620.6 13.4 %all-to-all-start = ((f32[2,128,512]{2,1,0:T(8,128)}), f32[2,128,512]{2,1,0:T(8,128)S(1)}, u32[]{:S(2)}, u32[]{:S(2)}) async-start(f32[2,128,512]{2,1,0:T(8,128)} %convolution_bitcast_fusion.1), calls=%async_computation | async-start | bytes 1048576 | tf_op jit(solution)/shard_map/all_to_all | solution.py:19
Sparse Core Ops, SparseCore 0:
  26.2 26.8 reduce-scatter.4
  55.6 326.6 reduce-scatter.2
  384.7 215.7 all-gather.1
where the time goes:
time: 642 us; the launch traced here: 641 us
  waiting for transfers between devices  578 us (90%)
  matrix products  24.3 us (4%)
  between operations  13.8 us (2%)
  local copies, waits for them, and re-layouts  10.2 us (2%)
  starting transfers between devices  9.33 us (1%)
    reduce_scatter x1, waiting for transfers between devices, sum_by_chip_2(): return lax.psum_scatter(parts, chips, scatter_dimension=0, tiled=True)[0]  329 us
    all_gather x1, waiting for transfers between devices, on_device(): weights = lax.all_gather(shard_bf, DP, axis=0, tiled=True)  217 us
    reduce_scatter x1, waiting for transfers between devices, sum_by_chip_2(): parts = lax.psum_scatter(parts, core, scatter_dimension=0, tiled=True)  27 us
  transfers between devices with their start and end apart: 5, of which 4 were waited for; matrix products, arithmetic and copies ran while one was open for 2% of the time, Pallas kernels for 0%

commit v1 on v0

--- a/solution.py
+++ b/solution.py
@@ -37,7 +37,8 @@
 
 def on_device(gate_pre, up_pre, out_grad, master, moment_one, moment_two):
     shard_bf = master.astype(jnp.bfloat16)
-    weights = lax.all_gather(shard_bf, DP, axis=0, tiled=True)
+    repeated = jnp.stack([shard_bf] * lax.axis_size(DP))
+    weights = jnp.concatenate(lax.all_to_all(repeated, DP, 0, 0), axis=0)
     micro = gate_pre.shape[0]
     total = micro * gate_pre.shape[1] * lax.axis_size(DP)
     own_rows = master.shape[0]

time: 642 us -> 566 us (0.88)
  waiting for transfers between devices: 578 us -> 361 us
  blocking collectives: 0 us -> 141 us
    all_gather x1 -> x0, waiting for transfers between devices: 217 us -> none  [on_device(): weights = lax.all_gather(shard_bf, DP, axis=0, tiled=True)]
    all_to_all x0 -> x1, blocking collectives: none -> 141 us  [on_device(): weights = jnp.concatenate(lax.all_to_all(repeated, DP, 0, 0), axis=0)]
  transfers between devices with their start and end apart: 5 -> 4, of which waited for: 4 -> 3; matrix products, arithmetic and copies ran while one was open for 2% -> 2% of each run, Pallas kernels for 0% -> 0%
where the time goes in v1:
time: 566 us
  waiting for transfers between devices  361 us (64%)
  blocking collectives  141 us (25%)
  matrix products  21.7 us (4%)
  between operations  14.1 us (2%)
  local copies, waits for them, and re-layouts  13.1 us (2%)
  starting transfers between devices  9.12 us (2%)
  other arithmetic  5.81 us (1%)
    reduce_scatter x1, waiting for transfers between devices, sum_by_chip_2(): return lax.psum_scatter(parts, chips, scatter_dimension=0, tiled=True)[0]  329 us
    all_to_all x1, blocking collectives, on_device(): weights = jnp.concatenate(lax.all_to_all(repeated, DP, 0, 0), axis=0)  141 us
    reduce_scatter x1, waiting for transfers between devices, sum_by_chip_2(): parts = lax.psum_scatter(parts, core, scatter_dimension=0, tiled=True)  27 us
  transfers between devices with their start and end apart: 4, of which 3 were waited for; matrix products, arithmetic and copies ran while one was open for 2% of the time, Pallas kernels for 0%

profile of v1, /device:TPU:32, one launch (start us, length us, event | category | flops | bytes accessed | tf_op | source)
XLA Modules:
  0.0 566.0 jit_solution(6935990033090908916)
XLA Ops:
  7.2 0.0 copy-start.1
  7.2 0.0 copy-start.2
  7.2 0.0 copy-start.4
  7.2 0.0 reduce-scatter.5.cloned.1.call-start
  7.2 3.2 fusion.41
  10.5 0.0 copy-done.1
  10.5 6.0 %convolution_add_fusion = f32[2816,1024]{0,1:T(8,128)} fusion(f32[2816,1024]{0,1:T(8,128)S(1)} %fusion.41, bf16[2,128,1024]{2,1,0:T(8,128)(2,1)S(1)} %copy-done.4, bf16[2,128,2816]{2,1,0:T(8,128)(2,1)S(1)} %copy-done.1, bf16[2,128,2816]{2,1,0:T(8,128)(2,1)S(1)} %copy-done.2), kind=kOutput, calls=%fused_computation | convolution fusion | flops 743964672 | bytes 24772608 | tf_op jit(solution)/shard_map/dot_general | solution.py:33
  16.5 9.5 %copy.12 = f32[2,64,8,2816]{3,2,1,0:T(8,128)} copy(f32[2,64,8,2816]{3,2,0,1:T(8,128)} %bitcast.148) | data formatting | bytes 23068672 | tf_op jit(solution)/shard_map/add | solution.py:78
  26.0 0.0 reduce-scatter.5.cloned.1.call-update
  26.0 0.0 reduce-scatter.3.cloned.1.call-start
  26.1 27.0 %reduce-scatter.5.cloned.1.call-done = f32[64,8,2816]{2,1,0:T(8,128)} async-done(((f32[128,8,2816]{2,1,0:T(8,128)}), f32[64,8,2816]{2,1,0:T(8,128)}) %reduce-scatter.5.cloned.1.call-update) | async-done | bytes 5767184 | tf_op jit(solution)/shard_map/reduce_scatter | solution.py:28
  53.1 0.0 reduce-scatter.3.cloned.1.call-update
  53.1 329.2 %reduce-scatter.3.cloned.1.call-done = f32[1,8,2816]{2,1,0:T(8,128)} async-done(((f32[64,8,2816]{2,1,0:T(8,128)}), f32[1,8,2816]{2,1,0:T(8,128)}) %reduce-scatter.3.cloned.1.call-update) | async-done | bytes 90128 | tf_op jit(solution)/shard_map/reduce_scatter | solution.py:29
  382.3 0.0 copy-done.8
  382.3 1.6 multiply_subtract_fusion
  383.9 0.4 stack.16
  384.3 141.4 %all_to_all.15 = bf16[128,8,2816]{2,1,0:T(8,128)(2,1)S(1)} all-to-all(bf16[128,8,2816]{2,1,0:T(8,128)(2,1)S(1)} %stack.16), channel_id=1, replica_groups=mesh['dp_0'=4,'dp_1'=2,'dp_2'=8,'dp_3'=2,'rep'=2] {'dp_0','dp_1','dp_2',..., dimensions={0} | all-to-all | bytes 11534336 | tf_op jit(solution)/shard_map/all_to_all | solution.py:41
  525.7 2.5 copy-done
  528.1 2.8 convolution_bitcast_fusion
  530.9 4.1 all-to-all-start.2
  535.1 3.8 fusion
  538.9 0.0 slice-done
  538.9 0.1 slice-done.1
  539.0 0.4 copy-done.3
  539.4 0.1 copy-done.5
  539.5 3.1 fusion.44
  542.6 2.8 convolution_bitcast_fusion.1
  545.4 0.0 all-to-all-done.2
  545.4 4.9 all-to-all-start.1
  550.3 3.4 pad_maximum_fusion
  553.7 4.7 all-to-all-done.1
  558.4 0.7 pad_maximum_fusion.2
  (17 shorter events, 0.1 us)
Async XLA Ops:
  7.2 3.3 copy-start.1
  7.2 3.3 copy-start.2
  7.2 3.3 copy-start.4
  7.2 45.9 %reduce-scatter.5.cloned.1.call-start = ((), (), s32[]{:S(2)}) async-start(), calls=%async_computation.6 | async-start | bytes 17301504 | tf_op jit(solution)/shard_map/reduce_scatter | solution.py:28
  26.0 356.2 %reduce-scatter.3.cloned.1.call-start = ((), (), s32[]{:S(2)}) async-start(), calls=%async_computation.5 | async-start | bytes 5857280 | tf_op jit(solution)/shard_map/reduce_scatter | solution.py:29
  53.1 329.2 %copy-start.7 = (f32[8,2816]{1,0:T(8,128)S(1)}, f32[8,2816]{1,0:T(8,128)}, u32[]{:S(2)}) copy-start(f32[8,2816]{1,0:T(8,128)} %param.9) | copy-start | bytes 270340
  53.1 329.2 %copy-start.8 = (f32[8,2816]{1,0:T(8,128)S(1)}, f32[8,2816]{1,0:T(8,128)}, u32[]{:S(2)}) copy-start(f32[8,2816]{1,0:T(8,128)} %param.10) | copy-start | bytes 270340
  53.1 329.2 %copy-start.9 = (f32[8,2816]{1,0:T(8,128)S(1)}, f32[8,2816]{1,0:T(8,128)}, u32[]{:S(2)}) copy-start(f32[8,2816]{1,0:T(8,128)} %param.11) | copy-start | bytes 270340
  525.7 2.5 copy-start
  530.9 7.9 %slice-start = ((s8[5767168]{0:T(1024)(128)(4,1)}), s8[1572864]{0:T(1024)(128)(4,1)S(1)}, s32[]{:S(2)}) async-start(s8[5767168]{0:T(1024)(128)(4,1)} %bitcast.151), calls=%async_computation.7 | async-start | bytes 3145728
  530.9 14.5 %all-to-all-start.2 = ((f32[2,128,512]{2,1,0:T(8,128)}), f32[2,128,512]{2,1,0:T(8,128)S(1)}, u32[]{:S(2)}, u32[]{:S(2)}) async-start(f32[2,128,512]{2,1,0:T(8,128)} %convolution_bitcast_fusion), calls=%async_computation.2 | async-start | bytes 1048576 | tf_op jit(solution)/shard_map/all_to_all | solution.py:19
  535.1 3.9 slice-start.1
  535.1 4.4 copy-start.3
  535.1 4.5 copy-start.5
  545.4 4.9 copy-start.6
  545.4 13.0 %all-to-all-start.1 = ((f32[2,128,512]{2,1,0:T(8,128)}), f32[2,128,512]{2,1,0:T(8,128)S(1)}, u32[]{:S(2)}, u32[]{:S(2)}) async-start(f32[2,128,512]{2,1,0:T(8,128)} %convolution_bitcast_fusion.1), calls=%async_computation.1 | async-start | bytes 1048576 | tf_op jit(solution)/shard_map/all_to_all | solution.py:19
Sparse Core Ops, SparseCore 0:
  26.2 26.8 reduce-scatter.4
  55.6 326.6 reduce-scatter.2
